TPU v7x, 32 devices: a whole 2x2x4 slice. The times are simulated.
32 devices in a mesh: pair: 4 (over y, x), aux: 8 (over z, core).
Axes of the slice: x: 2, y: 2, z: 4, core: 2. Of those that a mesh axis runs over, the one named last changes fastest.
Arguments:
- same_panels: bfloat16 [32, 2, 112, 59904], P('aux', None, None, 'pair'), may hold values from -1 to 1
- opposite_panels: bfloat16 [32, 2, 112, 59904], P('aux', None, None, 'pair'), may hold values from -1 to 1
- same_amplitudes: bfloat16 [32, 112, 112], replicated, may hold values from -2 to 2
- opposite_amplitudes: bfloat16 [32, 112, 112], replicated, may hold values from -2 to 2
- same_energies: float32 [32, 2, 112], replicated, may hold values from 0.5 to 3
- opposite_energies: float32 [32, 2, 112], replicated, may hold values from 0.5 to 3
- same_ranks: int32 [32], replicated, may hold values from 48 to 112
- opposite_ranks: int32 [32], replicated, may hold values from 48 to 112
Outputs:
- same_residual: float32 [32, 112, 112], P('pair', 'aux')
- opposite_residual: float32 [32, 112, 112], P('pair', 'aux')
Inputs may be any that keep to these rules, and one draw needn't show every extreme that they name: `same_ranks`: slots at or beyond a pair's rank are padding. `opposite_ranks`: slots at or beyond a pair's rank are padding.
All inputs are finite; a program needn't handle non-finite values.
Results may differ from a plain program's by a relative error of at most 0.0013.
Values may be sent and summed in bfloat16 or wider, within the bound.
A program may use at most 128 MiB of HBM per device.

v0:
```python
import jax
import jax.numpy as jnp
from jax import lax
from jax.sharding import PartitionSpec as P


def slot_mask(ranks, slots):
    places = jnp.arange(slots, dtype=jnp.int32)
    return (places[None, :] < ranks[:, None]).astype(jnp.float32)


def masked_amplitudes(amplitudes, keep):
    outer = keep[:, :, None] * keep[:, None, :]
    return (amplitudes.astype(jnp.float32) * outer).astype(jnp.bfloat16)


def dressing_total(panels, masked):
    mixed = jnp.einsum("pab,pbn->pan", masked, panels[:, 1], preferred_element_type=jnp.float32)
    return jnp.sum(panels[:, 0].astype(jnp.float32) * mixed, axis=(0, 1))


def partial_terms(panels, coupling):
    exchange = jnp.einsum(
        "pan,pbn->pab", panels[:, 0], panels[:, 1], preferred_element_type=jnp.float32
    )
    scaled = (panels[:, 0].astype(jnp.float32) * coupling[None, None, :]).astype(jnp.bfloat16)
    coulomb = jnp.einsum("pan,pbn->pab", scaled, panels[:, 1], preferred_element_type=jnp.float32)
    return exchange + coulomb


def finish_rows(summed, amplitudes, energies, ranks, pair_start, row_start):
    count = summed.shape[0]
    rows = summed.shape[1]
    slots = amplitudes.shape[1]
    keep = slot_mask(lax.dynamic_slice_in_dim(ranks, pair_start, count, 0), slots)
    amplitude = lax.dynamic_slice_in_dim(amplitudes, pair_start, count, 0)
    masked = masked_amplitudes(amplitude, keep)
    masked_rows = lax.dynamic_slice_in_dim(masked, row_start, rows, 1).astype(jnp.float32)
    energy = lax.dynamic_slice_in_dim(energies, pair_start, count, 0)
    first_gap = lax.dynamic_slice_in_dim(energy[:, 0], row_start, rows, 1)
    keep_rows = lax.dynamic_slice_in_dim(keep, row_start, rows, 1)
    diagonal = (first_gap[:, :, None] + energy[:, 1][:, None, :]) * masked_rows
    return (summed + diagonal) * (keep_rows[:, :, None] * keep[:, None, :])


def local_masked(amplitudes, ranks, start, count):
    slots = amplitudes.shape[1]
    keep = slot_mask(lax.dynamic_slice_in_dim(ranks, start, count, 0), slots)
    return masked_amplitudes(lax.dynamic_slice_in_dim(amplitudes, start, count, 0), keep)


def body(
    same_panels,
    opposite_panels,
    same_amplitudes,
    opposite_amplitudes,
    same_energies,
    opposite_energies,
    same_ranks,
    opposite_ranks,
):
    block_count = same_panels.shape[0]
    pair_index = lax.axis_index("pair")
    aux_index = lax.axis_index("aux")
    owned = block_count * lax.axis_size("aux") // lax.axis_size("pair")
    rows = same_amplitudes.shape[1] // lax.axis_size("aux")
    start = aux_index * block_count
    same_masked = local_masked(same_amplitudes, same_ranks, start, block_count)
    opposite_masked = local_masked(opposite_amplitudes, opposite_ranks, start, block_count)
    partial_coupling = dressing_total(same_panels, same_masked) + dressing_total(
        opposite_panels, opposite_masked
    )
    coupling = lax.psum(partial_coupling, "aux")
    same_rows, opposite_rows = (
        lax.all_to_all(
            partial_terms(same_panels, coupling), "aux", split_axis=1, concat_axis=0, tiled=True
        ),
        lax.all_to_all(
            partial_terms(opposite_panels, coupling), "aux", split_axis=1, concat_axis=0, tiled=True
        ),
    )
    same_sum, opposite_sum = (
        lax.psum_scatter(same_rows, "pair", scatter_dimension=0, tiled=True),
        lax.psum_scatter(opposite_rows, "pair", scatter_dimension=0, tiled=True),
    )
    pair_start = pair_index * owned
    row_start = aux_index * rows
    same_residual = finish_rows(
        same_sum, same_amplitudes, same_energies, same_ranks, pair_start, row_start
    )
    opposite_residual = finish_rows(
        opposite_sum, opposite_amplitudes, opposite_energies, opposite_ranks, pair_start, row_start
    )
    return (same_residual, opposite_residual)


def solution(mesh):
    placed = (
        P("aux", None, None, "pair"),
        P("aux", None, None, "pair"),
        P(),
        P(),
        P(),
        P(),
        P(),
        P(),
    )
    return jax.shard_map(
        body,
        mesh=mesh,
        in_specs=placed,
        out_specs=(P("pair", "aux", None), P("pair", "aux", None)),
        check_vma=False,
    )
```

profile of v0, /device:TPU:0, one launch (start us, length us, event | category | flops | bytes accessed | tf_op | source)
XLA Modules:
  0.0 178.4 jit_solution(11435442703354790816)
XLA Ops:
  7.2 0.7 dynamic_slice.49
  8.0 0.7 dynamic_slice.51
  8.8 10.7 %fusion = f32[14976]{0:T(1024)S(1)} fusion(bf16[4,2,112,14976]{3,2,1,0:T(8,128)(2,1)} %param.8, f32[4,112]{1,0:T(4,128)S(1)} %fusion.52, bf16[32,112,112]{2,1,0:T(8,128)(2,1)} %param.10, s32[]{:T(128)S(6)} %select_n.6), kind=kOutput, calls=%fused_computation.4 | convolution fusion | flops 1523185024 | bytes 27015684 | tf_op jit(solution)/shard_map/pab,pbn->pan/dot_general | solution.py:18
  19.5 10.8 %fusion.2 = f32[14976]{0:T(1024)S(1)} fusion(bf16[4,2,112,14976]{3,2,1,0:T(8,128)(2,1)} %param.9, f32[4,112]{1,0:T(4,128)S(1)} %fusion.53, bf16[32,112,112]{2,1,0:T(8,128)(2,1)} %param.11, s32[]{:T(128)S(6)} %select_n.6), kind=kOutput, calls=%fused_computation.6 | convolution fusion | flops 1523185024 | bytes 27015684 | tf_op jit(solution)/shard_map/pab,pbn->pan/dot_general | solution.py:18
  30.3 30.8 %psum.7 = f32[14976]{0:T(1024)S(1)} all-reduce(f32[14976]{0:T(1024)S(1)} %add.78), channel_id=1, replica_groups=mesh['pair'=4,'aux'=8] {'aux'}, use_global_device_ids=true, to_apply=%region_2.0 | all-reduce | flops 14976 | bytes 119808 | tf_op jit(solution)/shard_map/psum | solution.py:73
  61.1 10.6 %fusion.6 = f32[4,112,112]{2,1,0:T(8,128)S(1)} fusion(f32[14976]{0:T(1024)S(1)} %psum.7, bf16[4,2,112,14976]{3,2,1,0:T(8,128)(2,1)} %param.8), kind=kOutput, calls=%fused_computation.9 | convolution fusion | flops 1522999296 | bytes 27097600 | tf_op jit(solution)/shard_map/pan,pbn->pab/dot_general | solution.py:27
  71.7 10.6 %fusion.32 = f32[4,112,112]{2,1,0:T(8,128)S(1)} fusion(f32[4,112,112]{2,1,0:T(8,128)S(1)} %fusion.6, bf16[4,2,112,14976]{3,2,1,0:T(8,128)(2,1)} %param.8), kind=kOutput, calls=%fused_computation.34 | convolution fusion | flops 1502921728 | bytes 27238400 | tf_op jit(solution)/shard_map/pan,pbn->pab/dot_general | solution.py:23
  82.3 0.8 copy.64
  83.1 3.6 %all-to-all-start = ((f32[4,112,112]{2,0,1:T(4,128)}), f32[4,112,112]{2,0,1:T(4,128)S(1)}, u32[]{:S(2)}, u32[]{:S(2)}) async-start(f32[4,112,112]{2,0,1:T(4,128)} %copy.64), calls=%async_computation | async-start | bytes 458752 | tf_op jit(solution)/shard_map/all_to_all | solution.py:75
  86.7 10.6 %fusion.4 = f32[4,112,112]{2,1,0:T(8,128)S(1)} fusion(f32[14976]{0:T(1024)S(1)} %psum.7, bf16[4,2,112,14976]{3,2,1,0:T(8,128)(2,1)} %param.9), kind=kOutput, calls=%fused_computation.8 | convolution fusion | flops 1522999296 | bytes 27097600 | tf_op jit(solution)/shard_map/pan,pbn->pab/dot_general | solution.py:27
  97.5 10.6 %fusion.37 = f32[4,112,112]{2,1,0:T(8,128)S(1)} fusion(f32[4,112,112]{2,1,0:T(8,128)S(1)} %fusion.4, bf16[4,2,112,14976]{3,2,1,0:T(8,128)(2,1)} %param.9), kind=kOutput, calls=%fused_computation.35 | convolution fusion | flops 1502921728 | bytes 27238400 | tf_op jit(solution)/shard_map/pan,pbn->pab/dot_general | solution.py:23
  109.0 0.8 copy.71
  109.7 0.8 constant_dynamic-slice_fusion.5
  110.6 4.8 %all-to-all-start.1 = ((f32[4,112,112]{2,0,1:T(4,128)}), f32[4,112,112]{2,0,1:T(4,128)S(1)}, u32[]{:S(2)}, u32[]{:S(2)}) async-start(f32[4,112,112]{2,0,1:T(4,128)} %copy.71), calls=%async_computation.2 | async-start | bytes 458752 | tf_op jit(solution)/shard_map/all_to_all | solution.py:78
  115.5 0.7 copy.65
  116.9 1.0 constant_dynamic-slice_fusion.4
  117.9 1.0 constant_dynamic-slice_fusion.9
  118.8 5.6 %all-to-all-done.1 = f32[4,112,112]{2,0,1:T(4,128)S(1)} async-done(((f32[4,112,112]{2,0,1:T(4,128)}), f32[4,112,112]{2,0,1:T(4,128)S(1)}, u32[]{:S(2)}, u32[]{:S(2)}) %all-to-all-start.1) | async-done | bytes 200736 | tf_op jit(solution)/shard_map/all_to_all | solution.py:78
  124.4 0.7 copy.72
  125.2 0.7 constant_dynamic-slice_fusion.6
  125.9 17.9 %reduce-scatter.3.cloned.1.call-done = f32[8,14,112]{2,0,1:T(8,128)} async-done(((f32[32,14,112]{2,0,1:T(8,128)}), f32[8,14,112]{2,0,1:T(8,128)}) %reduce-scatter.3.cloned.1.call-update) | async-done | bytes 50192 | tf_op jit(solution)/shard_map/reduce_scatter | solution.py:83
  143.9 1.6 multiply_multiply_fusion.1
  145.4 24.6 %reduce-scatter.5.cloned.1.call-done = f32[8,14,112]{2,0,1:T(8,128)} async-done(((f32[32,14,112]{2,0,1:T(8,128)}), f32[8,14,112]{2,0,1:T(8,128)}) %reduce-scatter.5.cloned.1.call-update) | async-done | bytes 50192 | tf_op jit(solution)/shard_map/reduce_scatter | solution.py:84
  170.1 1.6 multiply_multiply_fusion
  (27 shorter events, 2.0 us)
Async XLA Ops:
  82.3 15.0 %copy-start = (s32[32]{0:T(128)S(1)}, s32[32]{0:T(128)}, u32[]{:S(2)}) copy-start(s32[32]{0:T(128)} %param.14) | copy-start | bytes 388
  83.1 27.5 %all-to-all-start = ((f32[4,112,112]{2,0,1:T(4,128)}), f32[4,112,112]{2,0,1:T(4,128)S(1)}, u32[]{:S(2)}, u32[]{:S(2)}) async-start(f32[4,112,112]{2,0,1:T(4,128)} %copy.64), calls=%async_computation | async-start | bytes 458752 | tf_op jit(solution)/shard_map/all_to_all | solution.py:75
  97.3 11.6 %copy-start.1 = (s32[32]{0:T(128)S(1)}, s32[32]{0:T(128)}, u32[]{:S(2)}) copy-start(s32[32]{0:T(128)} %param.15) | copy-start | bytes 388
  110.6 13.8 %all-to-all-start.1 = ((f32[4,112,112]{2,0,1:T(4,128)}), f32[4,112,112]{2,0,1:T(4,128)S(1)}, u32[]{:S(2)}, u32[]{:S(2)}) async-start(f32[4,112,112]{2,0,1:T(4,128)} %copy.71), calls=%async_computation.2 | async-start | bytes 458752 | tf_op jit(solution)/shard_map/all_to_all | solution.py:78
  115.4 28.4 %reduce-scatter.3.cloned.1.call-start = ((), (), s32[]{:S(2)}) async-start(), calls=%async_computation.4 | async-start | bytes 286720 | tf_op jit(solution)/shard_map/reduce_scatter | solution.py:83
  116.2 53.8 %reduce-scatter.5.cloned.1.call-start = ((), (), s32[]{:S(2)}) async-start(), calls=%async_computation.5 | async-start | bytes 286720 | tf_op jit(solution)/shard_map/reduce_scatter | solution.py:84
Sparse Core Ops, SparseCore 0:
  119.0 24.7 reduce-scatter.2
  146.7 23.3 reduce-scatter.4
where the time goes:
time: 179 us; the launch traced here: 178 us
  matrix products  63.9 us (36%)
  waiting for transfers between devices  48.2 us (27%)
  blocking collectives  30.8 us (17%)
  between operations  14.2 us (8%)
  local copies, waits for them, and re-layouts  9.48 us (5%)
  starting transfers between devices  8.49 us (5%)
  other arithmetic  3.41 us (2%)
    psum x1, blocking collectives, body(): coupling = lax.psum(partial_coupling, 'aux')  30.8 us
    reduce_scatter x1, waiting for transfers between devices, body(): lax.psum_scatter(opposite_rows, 'pair', scatter_dimension=0, tiled=True)  24.6 us
    dot_general x2, matrix products, dressing_total(): jnp.einsum('pab,pbn->pan', masked, panels[:, 1], preferred_element_type=j...  21.5 us
    dot_general x2, matrix products, partial_terms(): jnp.einsum('pan,pbn->pab', panels[:, 0], panels[:, 1], preferred_element_...  21.2 us
    dot_general x2, matrix products, partial_terms(): jnp.einsum('pan,pbn->pab', scaled, panels[:, 1], preferred_element_type=j...  21.2 us
    reduce_scatter x1, waiting for transfers between devices, body(): lax.psum_scatter(same_rows, 'pair', scatter_dimension=0, tiled=True)  17.9 us
    all_to_all x1, waiting for transfers between devices, body(): lax.all_to_all(partial_terms(opposite_panels, coupling), 'aux', split_axi...  5.62 us
    all_to_all x1, starting transfers between devices, body(): lax.all_to_all(partial_terms(opposite_panels, coupling), 'aux', split_axi...  4.83 us
  transfers between devices with their start and end apart: 4, of which 3 were waited for; matrix products, arithmetic and copies ran while one was open for 17% of the time, Pallas kernels for 0%

commit v1 on v0

v1 whole, which is shorter than its diff:
```python
import functools

import jax
import jax.numpy as jnp
from jax import lax
from jax.experimental import pallas as pl
from jax.experimental.pallas import tpu as pltpu
from jax.sharding import PartitionSpec as P

LANES = 128
GROUP = 2


def slot_mask(ranks, slots):
    places = jnp.arange(slots, dtype=jnp.int32)
    return (places[None, :] < ranks[:, None]).astype(jnp.float32)


def masked_amplitudes(amplitudes, keep):
    outer = keep[:, :, None] * keep[:, None, :]
    return (amplitudes.astype(jnp.float32) * outer).astype(jnp.bfloat16)


def finish_rows(summed, amplitudes, energies, ranks, pair_start, row_start):
    count = summed.shape[0]
    rows = summed.shape[1]
    slots = amplitudes.shape[1]
    keep = slot_mask(lax.dynamic_slice_in_dim(ranks, pair_start, count, 0), slots)
    amplitude = lax.dynamic_slice_in_dim(amplitudes, pair_start, count, 0)
    masked = masked_amplitudes(amplitude, keep)
    masked_rows = lax.dynamic_slice_in_dim(masked, row_start, rows, 1).astype(jnp.float32)
    energy = lax.dynamic_slice_in_dim(energies, pair_start, count, 0)
    first_gap = lax.dynamic_slice_in_dim(energy[:, 0], row_start, rows, 1)
    keep_rows = lax.dynamic_slice_in_dim(keep, row_start, rows, 1)
    diagonal = (first_gap[:, :, None] + energy[:, 1][:, None, :]) * masked_rows
    return (summed + diagonal) * (keep_rows[:, :, None] * keep[:, None, :])


def local_masked(amplitudes, ranks, start, count):
    slots = amplitudes.shape[1]
    keep = slot_mask(lax.dynamic_slice_in_dim(ranks, start, count, 0), slots)
    return masked_amplitudes(lax.dynamic_slice_in_dim(amplitudes, start, count, 0), keep)


def rows_dot(first, second):
    return lax.dot_general(
        first, second, (((1,), (1,)), ((), ())), preferred_element_type=jnp.float32
    )


def kernel(
    plan,
    same_ref,
    opposite_ref,
    masked_ref,
    same_out,
    opposite_out,
    panel,
    total,
    partial,
    flat,
    share,
    arrived,
    gathered,
    out_a,
    in_a,
    out_b,
    in_b,
    load_sem,
    scatter_send,
    scatter_recv,
    gather_send,
    gather_recv,
    a_send,
    a_recv,
    b_send,
    b_recv,
):
    pairs, auxes, count, slots, steps, width, chunk = plan
    sources = (same_ref, opposite_ref)
    fold = auxes // pairs
    rows = slots // auxes
    block = 2 * count
    groups = block // GROUP
    me_pair = lax.axis_index("pair")
    me_aux = lax.axis_index("aux")

    def load(step, spin, pair):
        at = pl.ds(pl.multiple_of(step * width, LANES), width)
        return pltpu.make_async_copy(
            sources[spin].at[pair, :, :, at],
            panel.at[spin * count + pair, :, :, at],
            load_sem.at[step, spin * count + pair],
        )

    @pl.loop(0, steps)
    def _(step):
        @pl.loop(0, count)
        def _(pair):
            load(step, 0, pair).start()
            load(step, 1, pair).start()

    barrier = pltpu.get_barrier_semaphore()
    devices = pairs * auxes
    me = me_pair * auxes + me_aux

    @pl.loop(1, devices)
    def _(ahead):
        other = lax.rem(me + ahead, devices)
        pl.semaphore_signal(
            barrier,
            inc=1,
            device_id=(lax.div(other, auxes), lax.rem(other, auxes)),
            device_id_type=pl.DeviceIdType.MESH,
        )

    total[...] = jnp.zeros_like(total)
    flat[...] = jnp.zeros_like(flat)

    def lanes(step):
        return pl.ds(pl.multiple_of(step * width, LANES), width)

    def exchange(place, step):
        at = lanes(step)
        total[place] += rows_dot(panel[place, 0, :, at], panel[place, 1, :, at])

    def dress(place, step):
        at = lanes(step)
        mixed = jnp.dot(
            masked_ref[place], panel[place, 1, :, at], preferred_element_type=jnp.float32
        )
        product = panel[place, 0, :, at].astype(jnp.float32) * mixed
        return jnp.sum(product.reshape(slots // 8, 8, width), axis=0)

    @pl.loop(0, steps)
    def _(step):
        partial[...] = jnp.zeros_like(partial)

        @pl.loop(0, count - 1)
        def _(pair):
            load(step, 0, pair).wait()
            load(step, 1, pair).wait()
            partial[...] += dress(pair, step) + dress(count + pair, step)
            exchange(pair, step)
            exchange(count + pair, step)

        load(step, 0, count - 1).wait()
        load(step, 1, count - 1).wait()
        summed = partial[...] + dress(count - 1, step) + dress(block - 1, step)
        flat[:, lanes(step)] = jnp.sum(summed, axis=0, keepdims=True)

    for part in range(auxes):
        share[part] = flat[:, part * chunk : (part + 1) * chunk]

    pl.semaphore_wait(barrier, devices - 1)

    def peer_aux(ahead):
        return lax.rem(me_aux + ahead, auxes)

    def scatter(ahead):
        other = peer_aux(ahead)
        return pltpu.make_async_remote_copy(
            src_ref=share.at[other],
            dst_ref=arrived.at[ahead],
            send_sem=scatter_send.at[ahead],
            recv_sem=scatter_recv.at[ahead],
            device_id=(me_pair, other),
            device_id_type=pl.DeviceIdType.MESH,
        )

    def gather(ahead):
        return pltpu.make_async_remote_copy(
            src_ref=gathered.at[me_aux],
            dst_ref=gathered.at[me_aux],
            send_sem=gather_send.at[ahead],
            recv_sem=gather_recv.at[ahead],
            device_id=(me_pair, peer_aux(ahead)),
            device_id_type=pl.DeviceIdType.MESH,
        )

    def gather_arrival(ahead):
        source = lax.rem(me_aux + auxes - ahead, auxes)
        return pltpu.make_async_remote_copy(
            src_ref=gathered.at[source],
            dst_ref=gathered.at[source],
            send_sem=gather_send.at[ahead],
            recv_sem=gather_recv.at[ahead],
            device_id=(me_pair, source),
            device_id_type=pl.DeviceIdType.MESH,
        )

    for ahead in range(1, auxes):
        scatter(ahead).start()

    @pl.loop(0, steps)
    def _(step):
        exchange(count - 1, step)

    mine = share[me_aux]
    for ahead in range(1, auxes):
        scatter(ahead).wait_recv()
        mine = mine + arrived[ahead]
    gathered[me_aux] = mine
    for ahead in range(1, auxes):
        gather(ahead).start()

    @pl.loop(0, steps)
    def _(step):
        exchange(block - 1, step)

    for ahead in range(1, auxes):
        gather_arrival(ahead).wait_recv()
    for part in range(auxes):
        flat[:, part * chunk : (part + 1) * chunk] = gathered[part]

    def send_a(group, ahead):
        other = lax.rem(me_pair + ahead, pairs)
        return pltpu.make_async_remote_copy(
            src_ref=out_a.at[other, group],
            dst_ref=in_a.at[ahead, group],
            send_sem=a_send.at[ahead, group],
            recv_sem=a_recv.at[ahead, group],
            device_id=(other, me_aux),
            device_id_type=pl.DeviceIdType.MESH,
        )

    owner = lax.div(me_aux, fold)
    slot = lax.rem(me_aux, fold)

    def send_b(group, part):
        return pltpu.make_async_remote_copy(
            src_ref=out_b.at[group, part],
            dst_ref=in_b.at[slot, group],
            send_sem=b_send.at[part, group],
            recv_sem=b_recv.at[slot, group],
            device_id=(owner, me_pair * fold + part),
            device_id_type=pl.DeviceIdType.MESH,
        )

    def stays(part):
        return jnp.logical_and(owner == me_pair, me_pair * fold + part == me_aux)

    def from_here(part):
        return jnp.logical_and(
            lax.div(me_aux, fold) == me_pair, me_pair * fold + part == me_aux
        )

    def arrival_b(group, part):
        return pltpu.make_async_remote_copy(
            src_ref=out_b.at[group, part],
            dst_ref=in_b.at[part, group],
            send_sem=b_send.at[part, group],
            recv_sem=b_recv.at[part, group],
            device_id=(owner, me_pair * fold + part),
            device_id_type=pl.DeviceIdType.MESH,
        )

    def forward(group):
        held = out_a[me_pair, group]
        for ahead in range(1, pairs):
            send_a(group, ahead).wait_recv()
            held = held + in_a[ahead, group]
        out_b[group] = held
        for part in range(fold):

            @pl.when(jnp.logical_not(stays(part)))
            def _():
                send_b(group, part).start()

            @pl.when(stays(part))
            def _():
                in_b[part, group] = out_b[group, part]

    for group in range(groups):
        for inner in range(GROUP):
            place = group * GROUP + inner

            @pl.loop(0, steps)
            def _(step):
                at = lanes(step)
                scaled = (panel[place, 0, :, at].astype(jnp.float32) * flat[:, at]).astype(
                    jnp.bfloat16
                )
                total[place] += rows_dot(scaled, panel[place, 1, :, at])

            value = total[place]
            for quarter in range(pairs):
                for part in range(fold):
                    first = (quarter * fold + part) * rows
                    out_a[quarter, group, part, inner, 0:rows, 0:slots] = value[
                        first : first + rows, :
                    ]
        for ahead in range(1, pairs):
            send_a(group, ahead).start()
        if group > 0:
            forward(group - 1)
    forward(groups - 1)

    outs = (same_out, opposite_out)
    for group in range(groups):
        for part in range(fold):

            @pl.when(jnp.logical_not(from_here(part)))
            def _():
                arrival_b(group, part).wait_recv()

            for inner in range(GROUP):
                place = group * GROUP + inner
                outs[place // count][part * count + place % count] = in_b[part, group, inner]

    for ahead in range(1, auxes):
        scatter(ahead).wait_send()
        gather(ahead).wait_send()
    for group in range(groups):
        for ahead in range(1, pairs):
            send_a(group, ahead).wait_send()
        for part in range(fold):

            @pl.when(jnp.logical_not(stays(part)))
            def _():
                send_b(group, part).wait_send()


def residual_sums(same_panels, opposite_panels, masked, pairs, auxes):
    if same_panels.shape[3] % LANES:
        extra = ((0, 0), (0, 0), (0, 0), (0, -same_panels.shape[3] % (8 * LANES)))
        same_panels = jnp.pad(same_panels, extra)
        opposite_panels = jnp.pad(opposite_panels, extra)
    count, _, slots, length = same_panels.shape
    tiles = length // LANES
    steps = next(parts for parts in range(min(8, tiles), tiles + 1) if tiles % parts == 0)
    width = length // steps
    chunk = -(-tiles // (8 * auxes)) * 8 * LANES
    fold = auxes // pairs
    rows = slots // auxes
    tall = -(-rows // 8) * 8
    wide = -(-slots // LANES) * LANES
    block = 2 * count
    groups = block // GROUP
    plan = (pairs, auxes, count, slots, steps, width, chunk)
    piece = (GROUP, tall, wide)
    shape = jax.ShapeDtypeStruct((count * fold, tall, wide), jnp.float32)
    anywhere = pl.BlockSpec(memory_space=pl.ANY)
    vmem = pl.BlockSpec(memory_space=pltpu.VMEM)
    dma = pltpu.SemaphoreType.DMA
    return pl.pallas_call(
        functools.partial(kernel, plan),
        out_shape=(shape, shape),
        in_specs=[anywhere, anywhere, vmem],
        out_specs=(vmem, vmem),
        scratch_shapes=[
            pltpu.VMEM((block, 2, slots, length), jnp.bfloat16),
            pltpu.VMEM((block, slots, slots), jnp.float32),
            pltpu.VMEM((8, width), jnp.float32),
            pltpu.VMEM((1, auxes * chunk + 8 * LANES), jnp.float32),
            pltpu.VMEM((auxes, 1, chunk), jnp.float32),
            pltpu.VMEM((auxes, 1, chunk), jnp.float32),
            pltpu.VMEM((auxes, 1, chunk), jnp.float32),
            pltpu.VMEM((pairs, groups, fold) + piece, jnp.float32),
            pltpu.VMEM((pairs, groups, fold) + piece, jnp.float32),
            pltpu.VMEM((groups, fold) + piece, jnp.float32),
            pltpu.VMEM((fold, groups) + piece, jnp.float32),
            dma((steps, block)),
            dma((auxes,)),
            dma((auxes,)),
            dma((auxes,)),
            dma((auxes,)),
            dma((pairs, groups)),
            dma((pairs, groups)),
            dma((fold, groups)),
            dma((fold, groups)),
        ],
        compiler_params=pltpu.CompilerParams(
            collective_id=0, has_side_effects=True, vmem_limit_bytes=67043328
        ),
        name="residual_sums",
    )(same_panels, opposite_panels, masked)


def body(
    pairs,
    auxes,
    same_panels,
    opposite_panels,
    same_amplitudes,
    opposite_amplitudes,
    same_energies,
    opposite_energies,
    same_ranks,
    opposite_ranks,
):
    count = same_panels.shape[0]
    pair_index = lax.axis_index("pair")
    aux_index = lax.axis_index("aux")
    owned = count * auxes // pairs
    rows = same_amplitudes.shape[1] // auxes
    start = aux_index * count
    masked = jnp.concatenate(
        [
            local_masked(same_amplitudes, same_ranks, start, count),
            local_masked(opposite_amplitudes, opposite_ranks, start, count),
        ]
    )
    same_sum, opposite_sum = residual_sums(same_panels, opposite_panels, masked, pairs, auxes)
    same_sum = same_sum[:, :rows, : same_amplitudes.shape[1]]
    opposite_sum = opposite_sum[:, :rows, : same_amplitudes.shape[1]]
    pair_start = pair_index * owned
    row_start = aux_index * rows
    same_residual = finish_rows(
        same_sum, same_amplitudes, same_energies, same_ranks, pair_start, row_start
    )
    opposite_residual = finish_rows(
        opposite_sum, opposite_amplitudes, opposite_energies, opposite_ranks, pair_start, row_start
    )
    return (same_residual, opposite_residual)


def solution(mesh):
    placed = (P("aux", None, None, "pair"),) * 2 + (P(),) * 6
    return jax.shard_map(
        functools.partial(body, mesh.shape["pair"], mesh.shape["aux"]),
        mesh=mesh,
        in_specs=placed,
        out_specs=(P("pair", "aux", None), P("pair", "aux", None)),
        check_vma=False,
    )
```

time: 179 us -> 73.5 us (0.41)
  the two profiles are of different devices: /device:TPU:0 before, /device:TPU:7 now
where the time goes in v1:
time: 73.5 us; the launch traced here: 73.1 us
  Pallas kernels  62.5 us (85%)
  local copies, waits for them, and re-layouts  5.8 us (8%)
  other arithmetic  4.05 us (6%)
    pallas_call x1, Pallas kernels, residual_sums(): pl.pallas_call(functools.partial(kernel, plan), out_shape=(shape, shape),...  62.5 us
    mul x2, other arithmetic, finish_rows(): return (summed + diagonal) * (keep_rows[:, :, None] * keep[:, None, :])  1.89 us

profile of v1, /device:TPU:7, one launch (start us, length us, event | category | flops | bytes accessed | tf_op | source)
XLA Modules:
  0.0 73.1 jit_solution(18121182581298998214)
XLA Ops:
  0.6 0.7 %dynamic_slice.49 = s32[4]{0:T(128)S(1)} dynamic-slice(s32[32]{0:T(128)} %param.14, s32[]{:T(128)S(6)} %select_n.6), dynamic_slice_sizes={4} | dynamic-slice | bytes 36 | tf_op jit(solution)/shard_map/dynamic_slice | solution.py:41
  1.4 0.1 fusion.4
  1.4 0.7 dynamic_slice.51
  2.2 0.1 fusion.5
  2.2 1.1 %multiply_convert_fusion = (bf16[4,112,112]{2,1,0:T(8,128)(2,1)S(1)}, bf16[4,112,112]{2,1,0:T(8,128)(2,1)S(1)}) fusion(f32[4,112]{1,0:T(4,128)S(1)} %fusion.5, bf16[32,112,112]{2,1,0:T(8,128)(2,1)} %param.11, s32[]{:T(128)S(6)} %select_n.6, f32[4,112]{1,0:T(4,128)S(1)} %fusion.4, bf16[32,112,112]{2,1,0:T(8,128)(2,1)} %param.10), kind=kLoop, calls=%fused_computation.1 | loop fusion | flops 401408 | bytes 409604 | tf_op jit(solution)/shard_map/convert_element_type | solution.py:21
  3.4 0.7 pad_maximum_fusion.masked_ref
  4.1 62.5 %residual_sums.1 = (f32[8,16,128]{2,1,0:T(8,128)}, f32[8,16,128]{2,1,0:T(8,128)}) custom-call(bf16[4,2,112,14976]{3,2,1,0:T(8,128)(2,1)} %same_ref.1, bf16[4,2,112,14976]{3,2,1,0:T(8,128)(2,1)} %opposite_ref.1, bf16[8,112,112]{2,1,0:T(8,128)(2,1)} %pad_maximum_fusion.masked_ref), custom_call_target="tpu_custom_call" | custom-call | tf_op jit(solution)/shard_map/residual_sums/pallas_call | solution.py:346
  66.7 0.7 %dynamic_slice.55 = s32[8]{0:T(128)S(1)} dynamic-slice(s32[32]{0:T(128)} %param.14, s32[]{:T(128)S(6)} %select_n.7), dynamic_slice_sizes={8} | dynamic-slice | bytes 68 | tf_op jit(solution)/shard_map/dynamic_slice | solution.py:28
  67.4 0.1 fusion.2
  67.5 0.7 dynamic_slice.61
  68.2 0.1 fusion.3
  68.3 0.1 constant_dynamic-slice_fusion
  68.3 0.8 %constant_dynamic-slice_fusion.1 = (f32[8,1,14]{2,1,0:T(1,128)S(1)}, f32[8,1,14]{2,1,0:T(1,128)S(1)}) fusion(f32[32,2,112]{2,1,0:T(2,128)} %param.13, s32[]{:T(128)S(6)} %select_n.7, s32[]{:T(128)S(6)} %select_n.8, f32[32,2,112]{2,1,0:T(2,128)} %param.12), kind=kLoop, calls=%fused_computation.14 | loop fusion | bytes 1800 | tf_op jit(solution)/shard_map/dynamic_slice | solution.py:33
  69.1 0.7 %constant_dynamic-slice_fusion.2 = (f32[8,1,112]{2,1,0:T(1,128)S(1)}, f32[8,1,112]{2,1,0:T(1,128)S(1)}) fusion(f32[32,2,112]{2,1,0:T(2,128)} %param.13, s32[]{:T(128)S(6)} %select_n.7, s32[]{:T(128)S(6)} %add.78, f32[32,2,112]{2,1,0:T(2,128)} %param.12), kind=kLoop, calls=%fused_computation.15 | loop fusion | bytes 14344 | tf_op jit(solution)/shard_map/slice | solution.py:35
  69.9 1.0 %multiply_multiply_fusion = f32[8,14,112]{2,1,0:T(8,128)S(1)} fusion(f32[8,16,128]{2,1,0:T(8,128)} %get-tuple-element.5, f32[8,112]{1,0:T(8,128)S(1)} %fusion.3, f32[8,14]{1,0:T(8,128)S(1)} %get-tuple-element.14, bf16[32,112,112]{2,1,0:T(8,128)(2,1)} %param.11, s32[]{:T(128)S(6)} %select_n.7, s32[]{:T(128)S(6)} %select_n.8, f32[8,112]{1,0:T(8,128)S(1)} %bitcast.17, ...), kind=kLoop, calls=%fused_computation.3 | loop fusion | flops 112896 | bytes 133512 | tf_op jit(solution)/shard_map/mul | solution.py:36
  70.8 0.6 copy.13
  71.5 0.9 %multiply_multiply_fusion.2 = f32[8,14,112]{2,1,0:T(8,128)S(1)} fusion(f32[8,16,128]{2,1,0:T(8,128)} %get-tuple-element.4, f32[8,112]{1,0:T(8,128)S(1)} %fusion.2, f32[8,14]{1,0:T(8,128)S(1)} %get-tuple-element.15, bf16[32,112,112]{2,1,0:T(8,128)(2,1)} %param.10, s32[]{:T(128)S(6)} %select_n.7, s32[]{:T(128)S(6)} %select_n.8, f32[8,112]{1,0:T(8,128)S(1)} %bitcast.15, ...), kind=kLoop, calls=%fused_computation.5 | loop fusion | flops 112896 | bytes 133512 | tf_op jit(solution)/shard_map/mul | solution.py:36
  72.4 0.6 copy.12
